TPU v7x, 256 devices: a whole 4x4x8 slice. The times are simulated.
256 devices in a mesh: row: 8 (over y_hi, x), col: 32 (over z, y_lo, core).
Axes of the slice: x: 4, y: 4 (y_hi: 2, y_lo: 2; y = y_hi * 2 + y_lo), z: 8, core: 2. Of those that a mesh axis runs over, the one named last changes fastest.
Arguments:
- legendre: bfloat16 [512, 512, 512], P('row', 'col'), may hold values from -6 to 6
- vectors: bfloat16 [512, 512, 256], P('row', 'col'), may hold values from -6 to 6
- panel_orders: int32 [8], replicated, may hold values from 0 to 511, as said below
- cycle_span: int32 [512, 2], replicated, may hold values from 0 to 2047, as said below
- cycle_weight: float32 [512], replicated, may hold values from 0.0009765625 to 0.0029296875
Outputs:
- projected: bfloat16 [512, 8, 256], P('col', 'row')
Inputs may be any that keep to these rules, and one draw needn't show every extreme that they name: `panel_orders`: the 8 entries are distinct orders; 0 and 511 are among them. `cycle_span`: in every cycle the first entry is smaller than the second.
All inputs are finite; a program needn't handle non-finite values.
Results may differ from a plain program's by a relative error of at most 0.008.
Values may be sent and summed in bfloat16 or wider, within the bound.
No kernel may reach another device: no remote copies, remote signals or barrier semaphores. Data moves between devices by JAX's collectives and lax.ppermute only.
A program may use at most 64 MiB of HBM per device.

v0:
```python
import math
import jax
import jax.numpy as jnp
from jax import lax
from jax.sharding import PartitionSpec as P

NPHI = 2048


def from_everyone(array, axis):
    copies = jnp.broadcast_to(array, (lax.axis_size(axis), *array.shape))
    return lax.all_to_all(copies, axis, split_axis=0, concat_axis=0, tiled=True)


def taken_together(array, axis):
    return from_everyone(array, axis).astype(jnp.float32).sum(axis=0)


def split_up(array, dim, length):
    before, after = (array.shape[:dim], array.shape[dim + 1 :])
    return jnp.moveaxis(array.reshape(*before, length, -1, *after), dim, 0)


def summed_on_arrival(array, axis, dim):
    length = lax.axis_size(axis)
    pieces = lax.all_to_all(split_up(array, dim, length), axis, 0, 0, tiled=True)
    return jnp.sum(pieces.astype(jnp.float32), axis=0)


def mask_coef(wavenumber, span_start, span_stop):
    cell_angle = 2.0 * math.pi / NPHI
    upper_sine = jnp.sin(cell_angle * (wavenumber * span_stop % NPHI).astype(jnp.float32))
    lower_sine = jnp.sin(cell_angle * (wavenumber * span_start % NPHI).astype(jnp.float32))
    half_angle = 2.0 * jnp.sin(math.pi / NPHI * wavenumber.astype(jnp.float32))
    safe_denom = jnp.where(wavenumber == 0, jnp.ones_like(half_angle), half_angle)
    span_width = cell_angle * (span_stop - span_start).astype(jnp.float32)
    return jnp.where(
        wavenumber == 0, span_width, cell_angle * (upper_sine - lower_sine) / safe_denom
    )


def cycle_mix(first_orders, col_orders, cycle_span, cycle_weight):
    span_start = cycle_span[:, 0][None, None, :]
    span_stop = cycle_span[:, 1][None, None, :]
    order_gap = jnp.abs(first_orders[:, None] - col_orders[None, :])[:, :, None]
    order_sum = (first_orders[:, None] + col_orders[None, :])[:, :, None]
    coef_sum = mask_coef(order_gap, span_start, span_stop) + mask_coef(
        order_sum, span_start, span_stop
    )
    return 0.5 * cycle_weight[None, None, :] * coef_sum


def per_device(legendre, vectors, panel_orders, cycle_span, cycle_weight):
    ord_count, deg_count, cycle_count = legendre.shape
    vec_count = vectors.shape[2]
    panel_count = panel_orders.shape[0]
    first_order = lax.axis_index("row") * ord_count
    first_degree = lax.axis_index("col") * deg_count
    local_orders = first_order + jnp.arange(ord_count, dtype=jnp.int32)
    local_degrees = first_degree + jnp.arange(deg_count, dtype=jnp.int32)
    keep_mask = local_degrees[None, :] >= local_orders[:, None]
    tables = jnp.where(keep_mask[:, :, None], legendre, jnp.zeros((), jnp.bfloat16))
    picker = (panel_orders[:, None] == local_orders[None, :]).astype(jnp.bfloat16)
    owned_terms = jnp.einsum("pi,ilj->plj", picker, legendre, preferred_element_type=jnp.float32)
    panel_keep = local_degrees[None, :] >= panel_orders[:, None]
    owned_terms = jnp.where(panel_keep[:, :, None], owned_terms, 0.0)
    summed = (
        taken_together(owned_terms.astype(jnp.bfloat16), "row")
        .astype(jnp.float32)
        .astype(jnp.bfloat16)
    )
    panel_rows = lax.all_gather(summed, "col", axis=1, tiled=True)
    mix_coef = cycle_mix(panel_orders, local_orders, cycle_span, cycle_weight)
    order_block = 8

    def add_block(block_index, running):
        block_start = block_index * order_block
        active = first_order + block_start <= first_degree + deg_count - 1

        def add_terms(partial_value):
            col_tables = lax.dynamic_slice_in_dim(tables, block_start, order_block, 0)
            cycle_coef = lax.dynamic_slice_in_dim(mix_coef, block_start, order_block, 1)
            vec_block = lax.dynamic_slice_in_dim(vectors, block_start, order_block, 0)
            vec_block = vec_block.reshape(order_block * deg_count, vec_count)
            weighted = (cycle_coef[:, :, None, :] * col_tables[None]).astype(jnp.bfloat16)
            weighted = weighted.reshape(panel_count, order_block * deg_count, cycle_count)
            panel_block = jnp.einsum(
                "plj,pqj->plq", panel_rows, weighted, preferred_element_type=jnp.float32
            )
            panel_block = panel_block.astype(jnp.bfloat16)
            return partial_value + jnp.einsum(
                "plq,qk->lpk", panel_block, vec_block, preferred_element_type=jnp.float32
            )

        def keep_terms(partial_value):
            return partial_value

        return lax.cond(active, add_terms, keep_terms, running)

    initial = jnp.zeros((panel_rows.shape[1], panel_count, vec_count), jnp.float32)
    whole_terms = lax.fori_loop(0, ord_count // order_block, add_block, initial)
    by_panel = summed_on_arrival(whole_terms.astype(jnp.bfloat16), "row", 1)
    result = summed_on_arrival(by_panel.astype(jnp.bfloat16), "col", 0)
    return result.astype(jnp.bfloat16)


def solution(mesh):
    in_specs = (P("row", "col", None), P("row", "col", None), P(), P(), P())
    out_specs = P("col", "row", None)
    return jax.shard_map(
        per_device, mesh=mesh, in_specs=in_specs, out_specs=out_specs, check_vma=False
    )
```

profile of v0, /device:TPU:1, one launch (start us, length us, event | category | flops | bytes accessed | tf_op | source)
XLA Modules:
  0.0 399.3 jit_solution(15246112433112409109)
XLA Ops:
  7.4 2.5 fusion.20
  10.0 23.6 %all_to_all.15 = bf16[8,8,16,512]{3,2,1,0:T(8,128)(2,1)S(1)} all-to-all(bf16[8,8,16,512]{3,2,1,0:T(8,128)(2,1)S(1)} %broadcast_in_dim.79), channel_id=1, replica_groups=mesh['row'=8,'col'=32] {'row'}, dimensions={0} | all-to-all | bytes 2097152 | tf_op jit(solution)/shard_map/all_to_all | solution.py:12
  34.9 1.3 broadcast_select_fusion
  36.2 65.4 %all-gather.2.cloned.1.call-done = bf16[8,512,512]{2,1,0:T(8,128)(2,1)} async-done(((bf16[8,16,512]{2,1,0:T(8,128)(2,1)}), bf16[8,512,512]{2,1,0:T(8,128)(2,1)}) %all-gather.2.cloned.1.call-update) | async-done | bytes 4194320 | tf_op jit(solution)/shard_map/all_gather | solution.py:72
  101.6 2.5 broadcast_in_dim.71
  104.1 133.4 %while.19 = (s32[]{:T(128)}, f32[512,8,256]{0,2,1:T(8,128)}, s32[]{:T(128)}, s32[]{:T(128)}, bf16[64,16,256]{2,1,0:T(8,128)(2,1)}, /*index=5*/bf16[64,16,512]{2,...) while((s32[]{:T(128)}, f32[512,8,256]{0,2,1:T(8,128)}, ...), condition=%wide.region_4.5_spmd.clone, body=%wide.region_1.4_spmd.clone.sunk | while | flops 823001088 | bytes 32586012 | solution.py:101
  105.2 2.8 fusion.32
  108.1 25.3 %conditional.3 = (f32[512,8,256]{0,2,1:T(8,128)}) conditional(s32[]{:T(128)} %convert_element_type.117, f32[512,8,256]{0,2,1:T(8,128)} %get-tuple-element.557, (s32[]{:T(128)}, bf16[64,16,256]{2,1,0:T(8,128)(2,1)}, f32[512]{0:T(512)S(1)}, bf16[64,16,512]{2,1,0:T(8,128)(2,1)}, bf16[8,512,512]{2,1,0:T(8,128)(2,1)}, ...), branch_computations={%region_2.2_spmd, %region_3.3_spmd.clone} | conditional | flops 809369600 | bytes 26283966 | solution.py:98
  110.1 14.6 %multiply_sine_fusion.3 = (f32[8,64,512]{2,1,0:T(8,128)S(1)}, f32[8,64,512]{2,1,0:T(8,128)S(1)}, f32[8,64,512]{2,1,0:T(8,128)S(1)}, f32[8,64,512]{2,1,0:T(8,128)S(1)}) fusion(f32[8,64,512]{2,1,0:T(8,128)S(1)} %get-tuple-element.343, f32[8,64,512]{2,1,0:T(8,128)S(1)} %get-tuple-element.344, f32[8,64,512]{2,1,0:T(8,128)} %get-tuple-element.349, ...), kind=kLoop, calls=%fused_computation.9 | loop fusion | flops 1048576 | bytes 9437184 | tf_op jit(solution)/shard_map/sin | solution.py:32
  125.9 7.5 %bitcast_add_fusion = f32[512,8,256]{0,2,1:T(8,128)} fusion(f32[512,8,256]{0,2,1:T(8,128)} %get-tuple-element.329, bf16[128,256,1]{1,0,2:T(8,128)(2,1)S(1)} %bitcast.39, bf16[8,128,512]{2,1,0:T(8,128)(2,1)S(1)} %fusion.2, bf16[8,512,512]{2,1,0:T(8,128)(2,1)} %get-tuple-element.333), kind=kOutput, calls=%fused_computation.1 | convolution fusion | flops 806879232 | bytes 13697024 | tf_op jit(solution)/shard_map/while/body/eval_jaxpr/cond/branch_1_fun/plq,qk->lpk/dot_general | solution.py:91
  134.5 2.8 fusion.32
  137.4 25.3 %conditional.3 = (f32[512,8,256]{0,2,1:T(8,128)}) conditional(s32[]{:T(128)} %convert_element_type.117, f32[512,8,256]{0,2,1:T(8,128)} %get-tuple-element.557, (s32[]{:T(128)}, bf16[64,16,256]{2,1,0:T(8,128)(2,1)}, f32[512]{0:T(512)S(1)}, bf16[64,16,512]{2,1,0:T(8,128)(2,1)}, bf16[8,512,512]{2,1,0:T(8,128)(2,1)}, ...), branch_computations={%region_2.2_spmd, %region_3.3_spmd.clone} | conditional | flops 809369600 | bytes 26283966 | solution.py:98
  139.4 14.6 %multiply_sine_fusion.3 = (f32[8,64,512]{2,1,0:T(8,128)S(1)}, f32[8,64,512]{2,1,0:T(8,128)S(1)}, f32[8,64,512]{2,1,0:T(8,128)S(1)}, f32[8,64,512]{2,1,0:T(8,128)S(1)}) fusion(f32[8,64,512]{2,1,0:T(8,128)S(1)} %get-tuple-element.343, f32[8,64,512]{2,1,0:T(8,128)S(1)} %get-tuple-element.344, f32[8,64,512]{2,1,0:T(8,128)} %get-tuple-element.349, ...), kind=kLoop, calls=%fused_computation.9 | loop fusion | flops 1048576 | bytes 9437184 | tf_op jit(solution)/shard_map/sin | solution.py:32
  155.2 7.5 %bitcast_add_fusion = f32[512,8,256]{0,2,1:T(8,128)} fusion(f32[512,8,256]{0,2,1:T(8,128)} %get-tuple-element.329, bf16[128,256,1]{1,0,2:T(8,128)(2,1)S(1)} %bitcast.39, bf16[8,128,512]{2,1,0:T(8,128)(2,1)S(1)} %fusion.2, bf16[8,512,512]{2,1,0:T(8,128)(2,1)} %get-tuple-element.333), kind=kOutput, calls=%fused_computation.1 | convolution fusion | flops 806879232 | bytes 13697024 | tf_op jit(solution)/shard_map/while/body/eval_jaxpr/cond/branch_1_fun/plq,qk->lpk/dot_general | solution.py:91
  163.8 2.8 fusion.32
  166.7 25.3 %conditional.3 = (f32[512,8,256]{0,2,1:T(8,128)}) conditional(s32[]{:T(128)} %convert_element_type.117, f32[512,8,256]{0,2,1:T(8,128)} %get-tuple-element.557, (s32[]{:T(128)}, bf16[64,16,256]{2,1,0:T(8,128)(2,1)}, f32[512]{0:T(512)S(1)}, bf16[64,16,512]{2,1,0:T(8,128)(2,1)}, bf16[8,512,512]{2,1,0:T(8,128)(2,1)}, ...), branch_computations={%region_2.2_spmd, %region_3.3_spmd.clone} | conditional | flops 809369600 | bytes 26283966 | solution.py:98
  168.7 14.6 %multiply_sine_fusion.3 = (f32[8,64,512]{2,1,0:T(8,128)S(1)}, f32[8,64,512]{2,1,0:T(8,128)S(1)}, f32[8,64,512]{2,1,0:T(8,128)S(1)}, f32[8,64,512]{2,1,0:T(8,128)S(1)}) fusion(f32[8,64,512]{2,1,0:T(8,128)S(1)} %get-tuple-element.343, f32[8,64,512]{2,1,0:T(8,128)S(1)} %get-tuple-element.344, f32[8,64,512]{2,1,0:T(8,128)} %get-tuple-element.349, ...), kind=kLoop, calls=%fused_computation.9 | loop fusion | flops 1048576 | bytes 9437184 | tf_op jit(solution)/shard_map/sin | solution.py:32
  184.5 7.5 %bitcast_add_fusion = f32[512,8,256]{0,2,1:T(8,128)} fusion(f32[512,8,256]{0,2,1:T(8,128)} %get-tuple-element.329, bf16[128,256,1]{1,0,2:T(8,128)(2,1)S(1)} %bitcast.39, bf16[8,128,512]{2,1,0:T(8,128)(2,1)S(1)} %fusion.2, bf16[8,512,512]{2,1,0:T(8,128)(2,1)} %get-tuple-element.333), kind=kOutput, calls=%fused_computation.1 | convolution fusion | flops 806879232 | bytes 13697024 | tf_op jit(solution)/shard_map/while/body/eval_jaxpr/cond/branch_1_fun/plq,qk->lpk/dot_general | solution.py:91
  193.1 2.8 fusion.32
  196.0 25.3 %conditional.3 = (f32[512,8,256]{0,2,1:T(8,128)}) conditional(s32[]{:T(128)} %convert_element_type.117, f32[512,8,256]{0,2,1:T(8,128)} %get-tuple-element.557, (s32[]{:T(128)}, bf16[64,16,256]{2,1,0:T(8,128)(2,1)}, f32[512]{0:T(512)S(1)}, bf16[64,16,512]{2,1,0:T(8,128)(2,1)}, bf16[8,512,512]{2,1,0:T(8,128)(2,1)}, ...), branch_computations={%region_2.2_spmd, %region_3.3_spmd.clone} | conditional | flops 809369600 | bytes 26283966 | solution.py:98
  198.0 14.6 %multiply_sine_fusion.3 = (f32[8,64,512]{2,1,0:T(8,128)S(1)}, f32[8,64,512]{2,1,0:T(8,128)S(1)}, f32[8,64,512]{2,1,0:T(8,128)S(1)}, f32[8,64,512]{2,1,0:T(8,128)S(1)}) fusion(f32[8,64,512]{2,1,0:T(8,128)S(1)} %get-tuple-element.343, f32[8,64,512]{2,1,0:T(8,128)S(1)} %get-tuple-element.344, f32[8,64,512]{2,1,0:T(8,128)} %get-tuple-element.349, ...), kind=kLoop, calls=%fused_computation.9 | loop fusion | flops 1048576 | bytes 9437184 | tf_op jit(solution)/shard_map/sin | solution.py:32
  213.8 7.5 %bitcast_add_fusion = f32[512,8,256]{0,2,1:T(8,128)} fusion(f32[512,8,256]{0,2,1:T(8,128)} %get-tuple-element.329, bf16[128,256,1]{1,0,2:T(8,128)(2,1)S(1)} %bitcast.39, bf16[8,128,512]{2,1,0:T(8,128)(2,1)S(1)} %fusion.2, bf16[8,512,512]{2,1,0:T(8,128)(2,1)} %get-tuple-element.333), kind=kOutput, calls=%fused_computation.1 | convolution fusion | flops 806879232 | bytes 13697024 | tf_op jit(solution)/shard_map/while/body/eval_jaxpr/cond/branch_1_fun/plq,qk->lpk/dot_general | solution.py:91
  222.4 2.8 fusion.32
  225.3 1.1 broadcast_in_dim.105
  226.4 2.8 fusion.32
  229.4 1.1 broadcast_in_dim.105
  230.5 2.8 fusion.32
  233.5 1.1 broadcast_in_dim.105
  234.6 2.8 fusion.32
  237.5 2.5 convert_bitcast_fusion
  240.0 19.9 %all_to_all.16 = bf16[8,512,1,256]{1,3,2,0:T(8,128)(2,1)S(1)} all-to-all(bf16[8,512,1,256]{1,3,2,0:T(8,128)(2,1)S(1)} %convert_bitcast_fusion), channel_id=1, replica_groups=mesh['row'=8,'col'=32] {'row'}, dimensions={0} | all-to-all | bytes 4194304 | tf_op jit(solution)/shard_map/all_to_all | solution.py:26
  260.3 131.5 %all_to_all.17 = bf16[32,16,1,256]{3,1,2,0:T(8,128)(2,1)S(1)} all-to-all(bf16[32,16,1,256]{3,1,2,0:T(8,128)(2,1)S(1)} %bitcast.40), channel_id=1, replica_groups=mesh['row'=8,'col'=32] {'col'}, dimensions={0} | all-to-all | bytes 524288 | tf_op jit(solution)/shard_map/all_to_all | solution.py:26
  (70 shorter events, 22.2 us)
Async XLA Ops:
  6.5 28.0 %copy-start.1 = (s32[8]{0:T(128)S(1)}, s32[8]{0:T(128)}, u32[]{:S(2)}) copy-start(s32[8]{0:T(128)} %param.11) | copy-start | bytes 100
  6.5 28.4 %copy-start = (bf16[64,16,512]{2,1,0:T(8,128)(2,1)S(1)}, bf16[64,16,512]{2,1,0:T(8,128)(2,1)}, u32[]{:S(2)}) copy-start(bf16[64,16,512]{2,1,0:T(8,128)(2,1)} %param.9) | copy-start | bytes 3145732
  6.5 28.1 %copy-start.2 = (s32[512,2]{0,1:T(2,128)S(1)}, s32[512,2]{0,1:T(2,128)}, u32[]{:S(2)}) copy-start(s32[512,2]{0,1:T(2,128)} %param.12) | copy-start | bytes 12292
  6.5 28.4 %copy-start.3 = (f32[512]{0:T(512)S(1)}, f32[512]{0:T(512)}, u32[]{:S(2)}) copy-start(f32[512]{0:T(512)} %param.13) | copy-start | bytes 6148
  6.5 95.1 %all-gather.2.cloned.1.call-start = ((), (), s32[]{:S(2)}) async-start(), calls=%async_computation.3 | async-start | bytes 4325376 | tf_op jit(solution)/shard_map/all_gather | solution.py:72
Sparse Core Ops, SparseCore 0:
  34.6 66.9 all-gather.1
where the time goes:
time: 400 us; the launch traced here: 399 us
  blocking collectives  175 us (44%)
  other arithmetic  92.4 us (23%)
  waiting for transfers between devices  65.4 us (16%)
  matrix products  32.4 us (8%)
  local copies, waits for them, and re-layouts  20 us (5%)
  between operations  13.5 us (3%)
    all_to_all x2, blocking collectives, summed_on_arrival(): lax.all_to_all(split_up(array, dim, length), axis, 0, 0, tiled=True)  151 us
    all_gather x1, waiting for transfers between devices, per_device(): panel_rows = lax.all_gather(summed, 'col', axis=1, tiled=True)  65.4 us
    sin x4, other arithmetic, mask_coef(): jnp.sin(cell_angle * (wavenumber * span_stop % NPHI).astype(jnp.float32))  58.4 us
    dot_general x4, matrix products, add_terms(): jnp.einsum('plq,qk->lpk', panel_block, vec_block, preferred_element_type=...  29.9 us
    all_to_all x1, blocking collectives, from_everyone(): return lax.all_to_all(copies, axis, split_axis=0, concat_axis=0, tiled=True)  23.6 us
    convert_element_type x8, other arithmetic, mask_coef(): (wavenumber * span_start % NPHI).astype(jnp.float32)  22.5 us
    broadcast_in_dim x8, local copies, waits for them, and re-layouts, mask_coef(): jnp.where(wavenumber == 0, span_width, cell_angle * (upper_sine - lower_s...  8.66 us
  transfers between devices with their start and end apart: 1, of which 1 were waited for; matrix products, arithmetic and copies ran while one was open for 0% of the time, Pallas kernels for 0%

commit v1 on v0

--- a/solution.py
+++ b/solution.py
@@ -69,7 +69,9 @@
         .astype(jnp.float32)
         .astype(jnp.bfloat16)
     )
-    panel_rows = lax.all_gather(summed, "col", axis=1, tiled=True)
+    panel_rows = jnp.concatenate(
+        lax.all_to_all(jnp.stack([summed] * lax.axis_size("col")), "col", 0, 0), axis=1
+    )
     mix_coef = cycle_mix(panel_orders, local_orders, cycle_span, cycle_weight)
     order_block = 8
 

time: 400 us -> 429 us (1.073)
  waiting for transfers between devices: 65.4 us -> 92.4 us
  between operations: 13.5 us -> 0.11 us
  starting transfers between devices: 0.03 us -> 10.7 us
  local copies, waits for them, and re-layouts: 20 us -> 27.3 us
    all_to_all x0 -> x1, waiting for transfers between devices: none -> 92.4 us  [per_device(): lax.all_to_all(jnp.stack([summed] * lax.axis_size('col')), 'col', 0, 0)]
    all_gather x1 -> x0, waiting for transfers between devices: 65.4 us -> none  [per_device(): panel_rows = lax.all_gather(summed, 'col', axis=1, tiled=True)]
    all_to_all x0 -> x1, starting transfers between devices: none -> 10.7 us  [per_device(): lax.all_to_all(jnp.stack([summed] * lax.axis_size('col')), 'col', 0, 0)]
    all_to_all x0 -> x1, local copies, waits for them, and re-layouts: none -> 4.76 us  [per_device(): lax.all_to_all(jnp.stack([summed] * lax.axis_size('col')), 'col', 0, 0)]
where the time goes in v1:
time: 429 us; the launch traced here: 428 us
  blocking collectives  173 us (40%)
  waiting for transfers between devices  92.4 us (22%)
  other arithmetic  91.6 us (21%)
  matrix products  32.4 us (8%)
  local copies, waits for them, and re-layouts  27.3 us (6%)
  starting transfers between devices  10.7 us (2%)
    all_to_all x2, blocking collectives, summed_on_arrival(): lax.all_to_all(split_up(array, dim, length), axis, 0, 0, tiled=True)  149 us
    all_to_all x1, waiting for transfers between devices, per_device(): lax.all_to_all(jnp.stack([summed] * lax.axis_size('col')), 'col', 0, 0)  92.4 us
    sin x4, other arithmetic, mask_coef(): jnp.sin(cell_angle * (wavenumber * span_stop % NPHI).astype(jnp.float32))  58.4 us
    dot_general x4, matrix products, add_terms(): jnp.einsum('plq,qk->lpk', panel_block, vec_block, preferred_element_type=...  29.9 us
    all_to_all x1, blocking collectives, from_everyone(): return lax.all_to_all(copies, axis, split_axis=0, concat_axis=0, tiled=True)  23.6 us
    convert_element_type x8, other arithmetic, mask_coef(): (wavenumber * span_start % NPHI).astype(jnp.float32)  22.4 us
    all_to_all x1, starting transfers between devices, per_device(): lax.all_to_all(jnp.stack([summed] * lax.axis_size('col')), 'col', 0, 0)  10.7 us
    broadcast_in_dim x8, local copies, waits for them, and re-layouts, mask_coef(): jnp.where(wavenumber == 0, span_width, cell_angle * (upper_sine - lower_s...  8.69 us
  transfers between devices with their start and end apart: 1, of which 1 were waited for; matrix products, arithmetic and copies ran while one was open for 0% of the time, Pallas kernels for 0%

profile of v1, /device:TPU:1, one launch (start us, length us, event | category | flops | bytes accessed | tf_op | source)
XLA Modules:
  0.0 428.1 jit_solution(6770281893427655529)
XLA Ops:
  0.7 2.5 fusion.20
  3.4 23.6 %all_to_all.20 = bf16[8,8,16,512]{3,2,1,0:T(8,128)(2,1)S(1)} all-to-all(bf16[8,8,16,512]{3,2,1,0:T(8,128)(2,1)S(1)} %broadcast_in_dim.79), channel_id=1, replica_groups=mesh['row'=8,'col'=32] {'row'}, dimensions={0} | all-to-all | bytes 2097152 | tf_op jit(solution)/shard_map/all_to_all | solution.py:12
  27.2 2.5 stack.2
  29.7 10.7 %all-to-all-start.1 = ((bf16[32,8,16,512]{3,2,1,0:T(8,128)(2,1)}), bf16[32,8,16,512]{3,2,1,0:T(8,128)(2,1)}, u32[]{:S(2)}, u32[]{:S(2)}) async-start(bf16[32,8,16,512]{3,2,1,0:T(8,128)(2,1)} %stack.2), calls=%async_computation.1 | async-start | bytes 8388608 | tf_op jit(solution)/shard_map/all_to_all | solution.py:73
  40.8 1.3 broadcast_select_fusion
  42.1 92.4 %all-to-all-done.1 = bf16[32,8,16,512]{3,2,1,0:T(8,128)(2,1)} async-done(((bf16[32,8,16,512]{3,2,1,0:T(8,128)(2,1)}), bf16[32,8,16,512]{3,2,1,0:T(8,128)(2,1)}, u32[]{:S(2)}, u32[]{:S(2)}) %all-to-all-start.1) | async-done | bytes 4194336 | tf_op jit(solution)/shard_map/all_to_all | solution.py:73
  134.5 4.8 %copy.30 = bf16[32,8,16,512]{3,2,0,1:T(8,128)(2,1)} copy(bf16[32,8,16,512]{3,2,1,0:T(8,128)(2,1)} %all-to-all-done.1) | data formatting | bytes 8388608 | tf_op jit(solution)/shard_map/all_to_all | solution.py:73
  139.2 2.5 broadcast_in_dim.71
  141.7 133.3 %while.19 = (s32[]{:T(128)}, f32[512,8,256]{0,2,1:T(8,128)}, s32[]{:T(128)}, s32[]{:T(128)}, bf16[64,16,256]{2,1,0:T(8,128)(2,1)}, /*index=5*/bf16[64,16,512]{2,...) while((s32[]{:T(128)}, f32[512,8,256]{0,2,1:T(8,128)}, ...), condition=%wide.region_4.5_spmd.clone, body=%wide.region_1.4_spmd.clone.sunk | while | flops 823001088 | bytes 32586012 | solution.py:103
  142.8 2.8 fusion.32
  145.8 25.3 %conditional.3 = (f32[512,8,256]{0,2,1:T(8,128)}) conditional(s32[]{:T(128)} %convert_element_type.117, f32[512,8,256]{0,2,1:T(8,128)} %get-tuple-element.557, (s32[]{:T(128)}, bf16[64,16,256]{2,1,0:T(8,128)(2,1)}, f32[512]{0:T(512)S(1)}, bf16[64,16,512]{2,1,0:T(8,128)(2,1)}, bf16[8,512,512]{2,1,0:T(8,128)(2,1)}, ...), branch_computations={%region_2.2_spmd, %region_3.3_spmd.clone} | conditional | flops 809369600 | bytes 26283966 | solution.py:100
  147.7 14.6 %multiply_sine_fusion.3 = (f32[8,64,512]{2,1,0:T(8,128)S(1)}, f32[8,64,512]{2,1,0:T(8,128)S(1)}, f32[8,64,512]{2,1,0:T(8,128)S(1)}, f32[8,64,512]{2,1,0:T(8,128)S(1)}) fusion(f32[8,64,512]{2,1,0:T(8,128)S(1)} %get-tuple-element.343, f32[8,64,512]{2,1,0:T(8,128)S(1)} %get-tuple-element.344, f32[8,64,512]{2,1,0:T(8,128)} %get-tuple-element.349, ...), kind=kLoop, calls=%fused_computation.9 | loop fusion | flops 1048576 | bytes 9437184 | tf_op jit(solution)/shard_map/sin | solution.py:32
  163.5 7.5 %bitcast_add_fusion = f32[512,8,256]{0,2,1:T(8,128)} fusion(f32[512,8,256]{0,2,1:T(8,128)} %get-tuple-element.329, bf16[128,256,1]{1,0,2:T(8,128)(2,1)S(1)} %bitcast.43, bf16[8,128,512]{2,1,0:T(8,128)(2,1)S(1)} %fusion.2, bf16[8,512,512]{2,1,0:T(8,128)(2,1)} %get-tuple-element.333), kind=kOutput, calls=%fused_computation.1 | convolution fusion | flops 806879232 | bytes 13697024 | tf_op jit(solution)/shard_map/while/body/eval_jaxpr/cond/branch_1_fun/plq,qk->lpk/dot_general | solution.py:93
  172.1 2.8 fusion.32
  175.0 25.3 %conditional.3 = (f32[512,8,256]{0,2,1:T(8,128)}) conditional(s32[]{:T(128)} %convert_element_type.117, f32[512,8,256]{0,2,1:T(8,128)} %get-tuple-element.557, (s32[]{:T(128)}, bf16[64,16,256]{2,1,0:T(8,128)(2,1)}, f32[512]{0:T(512)S(1)}, bf16[64,16,512]{2,1,0:T(8,128)(2,1)}, bf16[8,512,512]{2,1,0:T(8,128)(2,1)}, ...), branch_computations={%region_2.2_spmd, %region_3.3_spmd.clone} | conditional | flops 809369600 | bytes 26283966 | solution.py:100
  177.0 14.6 %multiply_sine_fusion.3 = (f32[8,64,512]{2,1,0:T(8,128)S(1)}, f32[8,64,512]{2,1,0:T(8,128)S(1)}, f32[8,64,512]{2,1,0:T(8,128)S(1)}, f32[8,64,512]{2,1,0:T(8,128)S(1)}) fusion(f32[8,64,512]{2,1,0:T(8,128)S(1)} %get-tuple-element.343, f32[8,64,512]{2,1,0:T(8,128)S(1)} %get-tuple-element.344, f32[8,64,512]{2,1,0:T(8,128)} %get-tuple-element.349, ...), kind=kLoop, calls=%fused_computation.9 | loop fusion | flops 1048576 | bytes 9437184 | tf_op jit(solution)/shard_map/sin | solution.py:32
  192.8 7.5 %bitcast_add_fusion = f32[512,8,256]{0,2,1:T(8,128)} fusion(f32[512,8,256]{0,2,1:T(8,128)} %get-tuple-element.329, bf16[128,256,1]{1,0,2:T(8,128)(2,1)S(1)} %bitcast.43, bf16[8,128,512]{2,1,0:T(8,128)(2,1)S(1)} %fusion.2, bf16[8,512,512]{2,1,0:T(8,128)(2,1)} %get-tuple-element.333), kind=kOutput, calls=%fused_computation.1 | convolution fusion | flops 806879232 | bytes 13697024 | tf_op jit(solution)/shard_map/while/body/eval_jaxpr/cond/branch_1_fun/plq,qk->lpk/dot_general | solution.py:93
  201.4 2.8 fusion.32
  204.3 25.3 %conditional.3 = (f32[512,8,256]{0,2,1:T(8,128)}) conditional(s32[]{:T(128)} %convert_element_type.117, f32[512,8,256]{0,2,1:T(8,128)} %get-tuple-element.557, (s32[]{:T(128)}, bf16[64,16,256]{2,1,0:T(8,128)(2,1)}, f32[512]{0:T(512)S(1)}, bf16[64,16,512]{2,1,0:T(8,128)(2,1)}, bf16[8,512,512]{2,1,0:T(8,128)(2,1)}, ...), branch_computations={%region_2.2_spmd, %region_3.3_spmd.clone} | conditional | flops 809369600 | bytes 26283966 | solution.py:100
  206.3 14.6 %multiply_sine_fusion.3 = (f32[8,64,512]{2,1,0:T(8,128)S(1)}, f32[8,64,512]{2,1,0:T(8,128)S(1)}, f32[8,64,512]{2,1,0:T(8,128)S(1)}, f32[8,64,512]{2,1,0:T(8,128)S(1)}) fusion(f32[8,64,512]{2,1,0:T(8,128)S(1)} %get-tuple-element.343, f32[8,64,512]{2,1,0:T(8,128)S(1)} %get-tuple-element.344, f32[8,64,512]{2,1,0:T(8,128)} %get-tuple-element.349, ...), kind=kLoop, calls=%fused_computation.9 | loop fusion | flops 1048576 | bytes 9437184 | tf_op jit(solution)/shard_map/sin | solution.py:32
  222.1 7.5 %bitcast_add_fusion = f32[512,8,256]{0,2,1:T(8,128)} fusion(f32[512,8,256]{0,2,1:T(8,128)} %get-tuple-element.329, bf16[128,256,1]{1,0,2:T(8,128)(2,1)S(1)} %bitcast.43, bf16[8,128,512]{2,1,0:T(8,128)(2,1)S(1)} %fusion.2, bf16[8,512,512]{2,1,0:T(8,128)(2,1)} %get-tuple-element.333), kind=kOutput, calls=%fused_computation.1 | convolution fusion | flops 806879232 | bytes 13697024 | tf_op jit(solution)/shard_map/while/body/eval_jaxpr/cond/branch_1_fun/plq,qk->lpk/dot_general | solution.py:93
  230.7 2.8 fusion.32
  233.6 25.3 %conditional.3 = (f32[512,8,256]{0,2,1:T(8,128)}) conditional(s32[]{:T(128)} %convert_element_type.117, f32[512,8,256]{0,2,1:T(8,128)} %get-tuple-element.557, (s32[]{:T(128)}, bf16[64,16,256]{2,1,0:T(8,128)(2,1)}, f32[512]{0:T(512)S(1)}, bf16[64,16,512]{2,1,0:T(8,128)(2,1)}, bf16[8,512,512]{2,1,0:T(8,128)(2,1)}, ...), branch_computations={%region_2.2_spmd, %region_3.3_spmd.clone} | conditional | flops 809369600 | bytes 26283966 | solution.py:100
  235.6 14.6 %multiply_sine_fusion.3 = (f32[8,64,512]{2,1,0:T(8,128)S(1)}, f32[8,64,512]{2,1,0:T(8,128)S(1)}, f32[8,64,512]{2,1,0:T(8,128)S(1)}, f32[8,64,512]{2,1,0:T(8,128)S(1)}) fusion(f32[8,64,512]{2,1,0:T(8,128)S(1)} %get-tuple-element.343, f32[8,64,512]{2,1,0:T(8,128)S(1)} %get-tuple-element.344, f32[8,64,512]{2,1,0:T(8,128)} %get-tuple-element.349, ...), kind=kLoop, calls=%fused_computation.9 | loop fusion | flops 1048576 | bytes 9437184 | tf_op jit(solution)/shard_map/sin | solution.py:32
  251.4 7.5 %bitcast_add_fusion = f32[512,8,256]{0,2,1:T(8,128)} fusion(f32[512,8,256]{0,2,1:T(8,128)} %get-tuple-element.329, bf16[128,256,1]{1,0,2:T(8,128)(2,1)S(1)} %bitcast.43, bf16[8,128,512]{2,1,0:T(8,128)(2,1)S(1)} %fusion.2, bf16[8,512,512]{2,1,0:T(8,128)(2,1)} %get-tuple-element.333), kind=kOutput, calls=%fused_computation.1 | convolution fusion | flops 806879232 | bytes 13697024 | tf_op jit(solution)/shard_map/while/body/eval_jaxpr/cond/branch_1_fun/plq,qk->lpk/dot_general | solution.py:93
  260.0 2.8 fusion.32
  264.0 2.8 fusion.32
  268.1 2.8 fusion.32
  272.1 2.8 fusion.32
  275.1 2.5 convert_bitcast_fusion
  277.5 19.9 %all_to_all.21 = bf16[8,512,1,256]{1,3,2,0:T(8,128)(2,1)S(1)} all-to-all(bf16[8,512,1,256]{1,3,2,0:T(8,128)(2,1)S(1)} %convert_bitcast_fusion), channel_id=1, replica_groups=mesh['row'=8,'col'=32] {'row'}, dimensions={0} | all-to-all | bytes 4194304 | tf_op jit(solution)/shard_map/all_to_all | solution.py:26
  297.9 129.5 %all_to_all.22 = bf16[32,16,1,256]{3,1,2,0:T(8,128)(2,1)S(1)} all-to-all(bf16[32,16,1,256]{3,1,2,0:T(8,128)(2,1)S(1)} %bitcast.44), channel_id=1, replica_groups=mesh['row'=8,'col'=32] {'col'}, dimensions={0} | all-to-all | bytes 524288 | tf_op jit(solution)/shard_map/all_to_all | solution.py:26
  (71 shorter events, 24.7 us)
Async XLA Ops:
  29.6 10.8 %copy-start.1 = (s32[8]{0:T(128)S(1)}, s32[8]{0:T(128)}, u32[]{:S(2)}) copy-start(s32[8]{0:T(128)} %param.11) | copy-start | bytes 100
  29.6 10.8 %copy-start.2 = (s32[512,2]{0,1:T(2,128)S(1)}, s32[512,2]{0,1:T(2,128)}, u32[]{:S(2)}) copy-start(s32[512,2]{0,1:T(2,128)} %param.12) | copy-start | bytes 12292
  29.6 11.1 %copy-start.3 = (f32[512]{0:T(512)S(1)}, f32[512]{0:T(512)}, u32[]{:S(2)}) copy-start(f32[512]{0:T(512)} %param.13) | copy-start | bytes 6148
  29.7 11.2 %copy-start = (bf16[64,16,512]{2,1,0:T(8,128)(2,1)S(1)}, bf16[64,16,512]{2,1,0:T(8,128)(2,1)}, u32[]{:S(2)}) copy-start(bf16[64,16,512]{2,1,0:T(8,128)(2,1)} %param.9) | copy-start | bytes 3145732
  29.7 104.8 %all-to-all-start.1 = ((bf16[32,8,16,512]{3,2,1,0:T(8,128)(2,1)}), bf16[32,8,16,512]{3,2,1,0:T(8,128)(2,1)}, u32[]{:S(2)}, u32[]{:S(2)}) async-start(bf16[32,8,16,512]{3,2,1,0:T(8,128)(2,1)} %stack.2), calls=%async_computation.1 | async-start | bytes 8388608 | tf_op jit(solution)/shard_map/all_to_all | solution.py:73
